TPU v7x, 32 devices: a whole 2x2x4 slice. The times are simulated.
32 devices in a mesh: batch: 4 (over x, core), cache: 8 (over z, y).
Axes of the slice: x: 2, y: 2, z: 4, core: 2. Of those that a mesh axis runs over, the one named last changes fastest.
Arguments:
- hidden_in: bfloat16 [32, 4096], P('batch'), may hold values from -6 to 6
- attn_gain: bfloat16 [4096], replicated, may hold values from 0.25 to 1.75
- w_query: bfloat16 [4096, 4096], P(None, 'cache'), may hold values from -0.09375 to 0.09375
- w_key: bfloat16 [4096, 1024], P(None, 'cache'), may hold values from -0.09375 to 0.09375
- w_value: bfloat16 [4096, 1024], P(None, 'cache'), may hold values from -0.09375 to 0.09375
- key_cache: bfloat16 [32, 1024, 1024], P('batch', 'cache'), may hold values from -400 to 400, as said below
- value_cache: bfloat16 [32, 1024, 1024], P('batch', 'cache'), may hold values from -6 to 6
- write_pos: int32 [32], P('batch'), may hold values from 0 to 3071, as said below
- cache_len: int32 [32], P('batch'), may hold values from 0 to 1023, as said below
- w_out: bfloat16 [4096, 4096], P('cache'), may hold values from -0.125 to 0.125
- mlp_gain: bfloat16 [4096], replicated, may hold values from 0.25 to 1.75
- w_gate: bfloat16 [4096, 7168], P(None, 'cache'), may hold values from -0.09375 to 0.09375
- w_up: bfloat16 [4096, 7168], P(None, 'cache'), may hold values from -0.09375 to 0.09375
- w_down: bfloat16 [7168, 4096], P('cache'), may hold values from -0.09375 to 0.09375
Outputs:
- hidden_out: bfloat16 [32, 4096], P('batch', 'cache')
Inputs may be any that keep to these rules, and one draw needn't show every extreme that they name: `key_cache`: keys of earlier tokens are finite reals. `write_pos`: positions of the new tokens; the largest value occurs in every draw. cache_len never exceeds write_pos; both 0 and 1023 occur in every draw, and many sequences attend fewer than 1023 earlier tokens.
All inputs are finite; a program needn't handle non-finite values.
Results may differ from a plain program's by a relative error of at most 0.017.
Values may be sent and summed in bfloat16 or wider, within the bound.
A program may use at most 64 MiB of HBM per device.

v0:
```python
import jax
import jax.numpy as jnp
from jax import lax
from jax.sharding import PartitionSpec as P

HEADS = 32
KV_HEADS = 8
HEAD_DIM = 128


def combined_all(value, axis, join):
    pieces = jax.tree.map(lambda part: lax.all_gather(part, axis), value)
    head = jax.tree.map(lambda part: part[0], pieces)
    tail = jax.tree.map(lambda part: part[1:], pieces)
    running, _ = lax.scan(lambda running, piece: (join(running, piece), None), head, tail)
    return running


def rms_norm(values, gain):
    wide = values.astype(jnp.float32)
    spread = jnp.mean(wide * wide, axis=-1, keepdims=True)
    return (wide * lax.rsqrt(spread + 1e-05) * gain.astype(jnp.float32)).astype(jnp.bfloat16)


def rotate(heads, position):
    half = heads.shape[-1] // 2
    freq = 10000.0 ** (-(jnp.arange(half, dtype=jnp.float32) * 2.0 / heads.shape[-1]))
    angle = position.astype(jnp.float32)[:, None] * freq[None, :]
    cosine = jnp.cos(angle)[:, None, :]
    sine = jnp.sin(angle)[:, None, :]
    first = heads[..., :half]
    second = heads[..., half:]
    return jnp.concatenate(
        [first * cosine - second * sine, second * cosine + first * sine], axis=-1
    )


def per_device(
    hidden_in,
    attn_gain,
    w_query,
    w_key,
    w_value,
    key_cache,
    value_cache,
    write_pos,
    cache_len,
    w_out,
    mlp_gain,
    w_gate,
    w_up,
    w_down,
):
    seqs = hidden_in.shape[0]
    embedding_width = hidden_in.shape[1]
    ncache = lax.axis_size("cache")
    position_index = lax.axis_index("cache")
    slots_dev = key_cache.shape[1]
    window = slots_dev * ncache
    group = HEADS // KV_HEADS
    scale = 1.0 / HEAD_DIM**0.5
    feature_width = embedding_width // ncache
    normed = rms_norm(hidden_in, attn_gain)
    query_slice = jnp.dot(normed, w_query, preferred_element_type=jnp.float32).astype(jnp.bfloat16)
    key_part = jnp.dot(normed, w_key, preferred_element_type=jnp.float32).astype(jnp.bfloat16)
    value_part = jnp.dot(normed, w_value, preferred_element_type=jnp.float32).astype(jnp.bfloat16)
    query_raw, key_raw, value_new = (
        lax.all_gather(query_slice, "cache", axis=1, tiled=True),
        lax.all_gather(key_part, "cache", axis=1, tiled=True),
        lax.all_gather(value_part, "cache", axis=1, tiled=True),
    )
    query = rotate(query_raw.astype(jnp.float32).reshape(seqs, HEADS, HEAD_DIM), write_pos).astype(
        jnp.bfloat16
    )
    fresh_key_row = rotate(
        key_raw.astype(jnp.float32).reshape(seqs, KV_HEADS, HEAD_DIM), write_pos
    ).astype(jnp.bfloat16)
    value_heads = value_new.reshape(seqs, KV_HEADS, HEAD_DIM)
    slots = position_index * slots_dev + jnp.arange(slots_dev, dtype=jnp.int32)
    dist = (write_pos[:, None] - 1 - slots[None, :]) % window + 1
    valid = dist <= cache_len[:, None]
    owner = write_pos % window // slots_dev == position_index
    query_head_group = query.reshape(seqs, KV_HEADS, group, HEAD_DIM)
    keys = key_cache.reshape(seqs, slots_dev, KV_HEADS, HEAD_DIM)
    values = value_cache.reshape(seqs, slots_dev, KV_HEADS, HEAD_DIM)
    scores = (
        jnp.einsum("bkgd,bwkd->bkgw", query_head_group, keys, preferred_element_type=jnp.float32)
        * scale
    )
    own = (
        jnp.einsum(
            "vyjf,vyf->vyj", query_head_group, fresh_key_row, preferred_element_type=jnp.float32
        )
        * scale
    )
    scores = jnp.where(valid[:, None, None, :], scores, -1e30)
    own = jnp.where(owner[:, None, None], own, -1e30)
    top = jnp.maximum(jnp.max(scores, axis=-1), own)
    weights = jnp.where(valid[:, None, None, :], jnp.exp(scores - top[..., None]), 0.0)
    own_weight = jnp.where(owner[:, None, None], jnp.exp(own - top), 0.0)
    total = jnp.sum(weights, axis=-1) + own_weight
    own_low = lax.optimization_barrier(own_weight.astype(jnp.bfloat16)).astype(jnp.float32)
    reduced_total = jnp.einsum(
        "bkgw,bwkd->bkgd", weights.astype(jnp.bfloat16), values, preferred_element_type=jnp.float32
    )
    reduced_total = (
        reduced_total + own_low[..., None] * value_heads.astype(jnp.float32)[:, :, None, :]
    )
    top_flat = top.reshape(seqs, HEADS)
    total_flat = total.reshape(seqs, HEADS)
    summed_flat = reduced_total.reshape(seqs, HEADS, HEAD_DIM)

    def combine(first, second):
        top_a, total_a, sum_a = first
        top_b, total_b, sum_b = second
        larger = jnp.maximum(top_a, top_b)
        factor_a = jnp.exp(top_a - larger)
        factor_b = jnp.exp(top_b - larger)
        merged = sum_a * factor_a[..., None] + sum_b * factor_b[..., None]
        return (larger, total_a * factor_a + total_b * factor_b, merged)

    merged_top, merged_total, merged_sum = combined_all(
        (top_flat, total_flat, summed_flat), "cache", combine
    )
    attended_heads_joined = (
        (merged_sum / merged_total[..., None]).reshape(seqs, HEADS * HEAD_DIM).astype(jnp.bfloat16)
    )
    attended = lax.dynamic_slice_in_dim(
        attended_heads_joined, position_index * feature_width, feature_width, 1
    )
    projected = jnp.dot(attended, w_out, preferred_element_type=jnp.float32)
    projected_sum = lax.psum(projected.astype(jnp.bfloat16), "cache").astype(jnp.float32)
    mid = (hidden_in.astype(jnp.float32) + projected_sum).astype(jnp.bfloat16)
    normed_mid = rms_norm(mid, mlp_gain)
    mid_own = lax.dynamic_slice_in_dim(mid, position_index * feature_width, feature_width, 1)
    gate = jnp.dot(normed_mid, w_gate, preferred_element_type=jnp.float32)
    upper = jnp.dot(normed_mid, w_up, preferred_element_type=jnp.float32)
    act = (jax.nn.silu(gate) * upper).astype(jnp.bfloat16)
    down = jnp.dot(act, w_down, preferred_element_type=jnp.float32)
    down_own = lax.psum_scatter(
        down.astype(jnp.bfloat16), "cache", scatter_dimension=1, tiled=True
    ).astype(jnp.float32)
    return (mid_own.astype(jnp.float32) + down_own).astype(jnp.bfloat16)


def solution(mesh):
    in_specs = (
        P("batch", None),
        P(),
        P(None, "cache"),
        P(None, "cache"),
        P(None, "cache"),
        P("batch", "cache", None),
        P("batch", "cache", None),
        P("batch"),
        P("batch"),
        P("cache", None),
        P(),
        P(None, "cache"),
        P(None, "cache"),
        P("cache", None),
    )
    out_specs = P("batch", "cache")
    return jax.shard_map(
        per_device, mesh=mesh, in_specs=in_specs, out_specs=out_specs, check_vma=False
    )
```

profile of v0, /device:TPU:0, one launch (start us, length us, event | category | flops | bytes accessed | tf_op | source)
XLA Modules:
  0.0 322.8 jit_solution(18037857481685795102)
XLA Ops:
  6.6 0.8 convert_element_type.87
  7.4 1.0 fusion.22
  8.4 1.6 convolution_convert_fusion.4
  10.0 27.9 %all_gather.19 = bf16[8,1024]{1,0:T(8,128)(2,1)S(1)} all-gather(bf16[8,128]{1,0:T(8,128)(2,1)S(1)} %convolution_convert_fusion.4), channel_id=1, replica_groups=mesh['batch'=4,'cache'=8] {'cache'}, dimensions={1}, use_global_device_ids=true | all-gather | bytes 18432 | tf_op jit(solution)/shard_map/all_gather | solution.py:69
  37.9 0.7 fusion.62
  38.6 3.0 convolution_convert_fusion.2
  41.6 30.5 %all_gather.18 = bf16[8,4096]{1,0:T(8,128)(2,1)S(1)} all-gather(bf16[8,512]{1,0:T(8,128)(2,1)S(1)} %convolution_convert_fusion.2), channel_id=1, replica_groups=mesh['batch'=4,'cache'=8] {'cache'}, dimensions={1}, use_global_device_ids=true | all-gather | bytes 73728 | tf_op jit(solution)/shard_map/all_gather | solution.py:68
  73.1 1.3 fusion.63
  74.4 0.3 fusion.27
  74.9 0.3 convolution_convert_fusion.3
  75.2 26.1 %all_gather.22 = bf16[8,1024]{1,0:T(8,128)(2,1)S(1)} all-gather(bf16[8,128]{1,0:T(8,128)(2,1)S(1)} %convolution_convert_fusion.3), channel_id=1, replica_groups=mesh['batch'=4,'cache'=8] {'cache'}, dimensions={1}, use_global_device_ids=true | all-gather | bytes 18432 | tf_op jit(solution)/shard_map/all_gather | solution.py:70
  101.3 1.4 fusion.15
  103.1 30.9 %all_gather.21 = f32[8,8,32]{2,1,0:T(8,128)S(1)} all-gather(f32[1,8,32]{2,1,0:T(8,128)S(1)} %copy.37), channel_id=1, replica_groups=mesh['batch'=4,'cache'=8] {'cache'}, dimensions={0}, use_global_device_ids=true | all-gather | bytes 9216 | tf_op jit(solution)/shard_map/all_gather | solution.py:12
  134.0 30.6 %all_gather.20 = f32[8,8,32]{2,1,0:T(8,128)S(1)} all-gather(f32[1,8,32]{2,1,0:T(8,128)S(1)} %copy.35), channel_id=1, replica_groups=mesh['batch'=4,'cache'=8] {'cache'}, dimensions={0}, use_global_device_ids=true | all-gather | bytes 9216 | tf_op jit(solution)/shard_map/all_gather | solution.py:12
  164.7 1.2 slice.49
  165.9 0.9 slice_bitcast_fusion
  166.9 1.5 while.14
  168.5 3.5 %convolution_convert_fusion.1 = bf16[8,4096]{1,0:T(8,128)(2,1)} fusion(bf16[512,4096]{1,0:T(8,128)(2,1)} %param.25, bf16[8,4096]{1,0:T(8,128)(2,1)S(1)} %bitcast.80, s32[]{:T(128)S(6)} %select_n.47), kind=kOutput, calls=%fused_computation.9 | convolution fusion | flops 33587200 | bytes 4268036 | tf_op jit(solution)/shard_map/dot_general | solution.py:131
  172.0 67.0 %all-reduce.2.cloned.1.call-done = bf16[8,4096]{1,0:T(8,128)(2,1)} async-done(((bf16[8,4096]{1,0:T(8,128)(2,1)}), bf16[8,4096]{1,0:T(8,128)(2,1)}) %all-reduce.2.cloned.1.call-update) | async-done | bytes 65552 | tf_op jit(solution)/shard_map/psum | solution.py:132
  239.1 1.0 fusion.19
  240.1 4.2 %fusion.44 = f32[8,896]{1,0:T(8,128)S(1)} fusion(bf16[4096,896]{1,0:T(8,128)(2,1)} %param.27, bf16[8,4096]{1,0:T(8,128)(2,1)S(1)} %get-tuple-element.71, f32[4096]{0:T(1024)S(1)} %convert_element_type.105, f32[8]{0:T(128)S(1)} %add_rsqrt_fusion), kind=kOutput, calls=%fused_computation.67 | convolution fusion | flops 58851328 | bytes 7450656 | tf_op jit(solution)/shard_map/dot_general | solution.py:136
  244.2 8.1 %convolution_convert_fusion = bf16[8,4096]{1,0:T(8,128)(2,1)} fusion(bf16[896,4096]{1,0:T(8,128)(2,1)} %param.29, bf16[4096,896]{1,0:T(8,128)(2,1)} %param.28, f32[8,896]{1,0:T(8,128)S(1)} %fusion.44, bf16[8,4096]{1,0:T(8,128)(2,1)S(1)} %get-tuple-element.71, f32[4096]{0:T(1024)S(1)} %convert_element_type.105, f32[8]{0:T(128)S(1)} %add_rsqrt_fusion), kind=kOutput, calls=%fused_computation.8 | convolution fusion | flops 117647360 | bytes 14856224 | tf_op jit(solution)/shard_map/dot_general | solution.py:139
  252.4 62.5 %reduce-scatter.2.cloned.1.call-done = bf16[8,512]{1,0:T(8,128)(2,1)} async-done(((bf16[8,4096]{1,0:T(8,128)(2,1)}), bf16[8,512]{1,0:T(8,128)(2,1)}) %reduce-scatter.2.cloned.1.call-update) | async-done | bytes 8208 | tf_op jit(solution)/shard_map/reduce_scatter | solution.py:140
  314.9 1.3 add_convert_fusion.2
  (66 shorter events, 3.0 us)
Async XLA Ops:
  6.5 66.5 %copy-start = (bf16[8,128,1024]{2,1,0:T(8,128)(2,1)S(1)}, bf16[8,128,1024]{2,1,0:T(8,128)(2,1)}, u32[]{:S(2)}) copy-start(bf16[8,128,1024]{2,1,0:T(8,128)(2,1)} %param.21) | copy-start | bytes 6291460
  6.5 66.0 %copy-start.6 = (s32[8]{0:T(128)S(1)}, s32[8]{0:T(128)}, u32[]{:S(2)}) copy-start(s32[8]{0:T(128)} %param.23) | copy-start | bytes 100
  6.5 66.4 %copy-start.4 = (s32[8]{0:T(128)S(1)}, s32[8]{0:T(128)}, u32[]{:S(2)}) copy-start(s32[8]{0:T(128)} %param.24) | copy-start | bytes 100
  6.5 158.1 %all-gather.2.cloned.1.call-start = ((), (), s32[]{:S(2)}) async-start(), calls=%async_computation.1 | async-start | bytes 1179648 | tf_op jit(solution)/shard_map/all_gather | solution.py:12
  38.6 36.2 %copy-start.1 = (bf16[8,4096]{1,0:T(8,128)(2,1)S(1)}, bf16[8,4096]{1,0:T(8,128)(2,1)}, u32[]{:S(2)}) copy-start(bf16[8,4096]{1,0:T(8,128)(2,1)} %param.16) | copy-start | bytes 196612
  38.6 36.2 %copy-start.2 = (bf16[4096,128]{1,0:T(8,128)(2,1)S(1)}, bf16[4096,128]{1,0:T(8,128)(2,1)}, u32[]{:S(2)}) copy-start(bf16[4096,128]{1,0:T(8,128)(2,1)} %param.20) | copy-start | bytes 3145732
  72.6 28.7 %copy-start.5 = (bf16[8,128,1024]{2,1,0:T(8,128)(2,1)S(1)}, bf16[8,128,1024]{2,1,0:T(8,128)(2,1)}, u32[]{:S(2)}) copy-start(bf16[8,128,1024]{2,1,0:T(8,128)(2,1)} %param.22) | copy-start | bytes 6291460
  102.7 136.4 %all-reduce.2.cloned.1.call-start = ((), (), s32[]{:S(2)}) async-start(), calls=%async_computation.2 | async-start | bytes 131072 | tf_op jit(solution)/shard_map/psum | solution.py:132
  164.6 7.4 %copy-start.3 = (bf16[4096]{0:T(1024)(128)(2,1)S(1)}, bf16[4096]{0:T(1024)(128)(2,1)}, u32[]{:S(2)}) copy-start(bf16[4096]{0:T(1024)(128)(2,1)} %param.26) | copy-start | bytes 24580
  172.0 143.0 %reduce-scatter.2.cloned.1.call-start = ((), (), s32[]{:S(2)}) async-start(), calls=%async_computation.3 | async-start | bytes 73728 | tf_op jit(solution)/shard_map/reduce_scatter | solution.py:140
Sparse Core Ops, SparseCore 0:
  102.8 38.3 all-gather.1
  172.1 66.9 all-reduce.1
  252.5 62.3 reduce-scatter.1
where the time goes:
time: 323 us
  blocking collectives  146 us (45%)
  waiting for transfers between devices  130 us (40%)
  matrix products  23.6 us (7%)
  between operations  13.3 us (4%)
  other arithmetic  7.25 us (2%)
    psum x1, waiting for transfers between devices, per_device(): lax.psum(projected.astype(jnp.bfloat16), 'cache').astype(jnp.float32)  67 us
    reduce_scatter x1, waiting for transfers between devices, per_device(): lax.psum_scatter(down.astype(jnp.bfloat16), 'cache', scatter_dimension=1,...  62.5 us
    all_gather x2, blocking collectives, combined_all(): pieces = jax.tree.map(lambda part: lax.all_gather(part, axis), value)  61.5 us
    all_gather x1, blocking collectives, per_device(): lax.all_gather(query_slice, 'cache', axis=1, tiled=True)  30.5 us
    all_gather x1, blocking collectives, per_device(): lax.all_gather(key_part, 'cache', axis=1, tiled=True)  27.9 us
    all_gather x1, blocking collectives, per_device(): lax.all_gather(value_part, 'cache', axis=1, tiled=True)  26.1 us
    dot_general x1, matrix products, per_device(): down = jnp.dot(act, w_down, preferred_element_type=jnp.float32)  8.13 us
  transfers between devices with their start and end apart: 3, of which 2 were waited for; matrix products, arithmetic and copies ran while one was open for 0% of the time, Pallas kernels for 0%

commit v1 on v0

--- a/solution.py
+++ b/solution.py
@@ -129,7 +129,11 @@
         attended_heads_joined, position_index * feature_width, feature_width, 1
     )
     projected = jnp.dot(attended, w_out, preferred_element_type=jnp.float32)
-    projected_sum = lax.psum(projected.astype(jnp.bfloat16), "cache").astype(jnp.float32)
+
+    def push_ways(sample, bus_axis):
+        return jnp.sum(lax.all_gather(sample, bus_axis), axis=0)
+
+    projected_sum = push_ways(projected.astype(jnp.bfloat16), "cache").astype(jnp.float32)
     mid = (hidden_in.astype(jnp.float32) + projected_sum).astype(jnp.bfloat16)
     normed_mid = rms_norm(mid, mlp_gain)
     mid_own = lax.dynamic_slice_in_dim(mid, position_index * feature_width, feature_width, 1)

time: 323 us -> 284 us (0.88)
  waiting for transfers between devices: 130 us -> 60.4 us
  blocking collectives: 146 us -> 177 us
    psum x1 -> x0, waiting for transfers between devices: 67 us -> none  [per_device(): lax.psum(projected.astype(jnp.bfloat16), 'cache').astype(jnp.float32)]
    all_gather x0 -> x1, blocking collectives: none -> 31.3 us  [push_ways(): return jnp.sum(lax.all_gather(sample, bus_axis), axis=0)]
  transfers between devices with their start and end apart: 3 -> 2, of which waited for: 2 -> 1; matrix products, arithmetic and copies ran while one was open for 0% -> 0% of each run, Pallas kernels for 0% -> 0%
where the time goes in v1:
time: 284 us
  blocking collectives  177 us (62%)
  waiting for transfers between devices  60.4 us (21%)
  matrix products  22.9 us (8%)
  between operations  13.6 us (5%)
  other arithmetic  6.46 us (2%)
    all_gather x2, blocking collectives, combined_all(): pieces = jax.tree.map(lambda part: lax.all_gather(part, axis), value)  61.5 us
    reduce_scatter x1, waiting for transfers between devices, per_device(): lax.psum_scatter(down.astype(jnp.bfloat16), 'cache', scatter_dimension=1,...  60.3 us
    all_gather x1, blocking collectives, push_ways(): return jnp.sum(lax.all_gather(sample, bus_axis), axis=0)  31.3 us
    all_gather x1, blocking collectives, per_device(): lax.all_gather(query_slice, 'cache', axis=1, tiled=True)  30.5 us
    all_gather x1, blocking collectives, per_device(): lax.all_gather(key_part, 'cache', axis=1, tiled=True)  27.9 us
    all_gather x1, blocking collectives, per_device(): lax.all_gather(value_part, 'cache', axis=1, tiled=True)  26.1 us
    dot_general x1, matrix products, per_device(): down = jnp.dot(act, w_down, preferred_element_type=jnp.float32)  8.13 us
  transfers between devices with their start and end apart: 2, of which 1 were waited for; matrix products, arithmetic and copies ran while one was open for 0% of the time, Pallas kernels for 0%

profile of v1, /device:TPU:0, one launch (start us, length us, event | category | flops | bytes accessed | tf_op | source)
XLA Modules:
  0.0 283.6 jit_solution(3126488763599877186)
XLA Ops:
  6.6 0.8 convert_element_type.89
  7.4 1.0 fusion.22
  8.4 1.6 convolution_convert_fusion.4
  10.0 27.9 %all_gather.25 = bf16[8,1024]{1,0:T(8,128)(2,1)S(1)} all-gather(bf16[8,128]{1,0:T(8,128)(2,1)S(1)} %convolution_convert_fusion.4), channel_id=1, replica_groups=mesh['batch'=4,'cache'=8] {'cache'}, dimensions={1}, use_global_device_ids=true | all-gather | bytes 18432 | tf_op jit(solution)/shard_map/all_gather | solution.py:69
  37.9 0.7 fusion.62
  38.6 3.0 %convolution_convert_fusion.2 = bf16[8,512]{1,0:T(8,128)(2,1)S(1)} fusion(bf16[4096,512]{1,0:T(8,128)(2,1)} %param.18, bf16[8,4096]{1,0:T(8,128)(2,1)} %param.16, f32[4096]{0:T(1024)S(1)} %convert_element_type.89, f32[8]{0:T(128)S(1)} %add_rsqrt_fusion.1), kind=kOutput, calls=%fused_computation.21 | convolution fusion | flops 33689600 | bytes 4284448 | tf_op jit(solution)/shard_map/dot_general | solution.py:64
  41.6 30.5 %all_gather.24 = bf16[8,4096]{1,0:T(8,128)(2,1)S(1)} all-gather(bf16[8,512]{1,0:T(8,128)(2,1)S(1)} %convolution_convert_fusion.2), channel_id=1, replica_groups=mesh['batch'=4,'cache'=8] {'cache'}, dimensions={1}, use_global_device_ids=true | all-gather | bytes 73728 | tf_op jit(solution)/shard_map/all_gather | solution.py:68
  72.7 0.3 fusion.33
  73.1 1.3 fusion.63
  74.5 0.3 fusion.27
  74.9 0.3 convolution_convert_fusion.3
  75.2 26.1 %all_gather.28 = bf16[8,1024]{1,0:T(8,128)(2,1)S(1)} all-gather(bf16[8,128]{1,0:T(8,128)(2,1)S(1)} %convolution_convert_fusion.3), channel_id=1, replica_groups=mesh['batch'=4,'cache'=8] {'cache'}, dimensions={1}, use_global_device_ids=true | all-gather | bytes 18432 | tf_op jit(solution)/shard_map/all_gather | solution.py:70
  101.3 1.4 fusion.15
  103.1 30.9 %all_gather.27 = f32[8,8,32]{2,1,0:T(8,128)S(1)} all-gather(f32[1,8,32]{2,1,0:T(8,128)S(1)} %copy.37), channel_id=1, replica_groups=mesh['batch'=4,'cache'=8] {'cache'}, dimensions={0}, use_global_device_ids=true | all-gather | bytes 9216 | tf_op jit(solution)/shard_map/all_gather | solution.py:12
  134.0 30.6 %all_gather.26 = f32[8,8,32]{2,1,0:T(8,128)S(1)} all-gather(f32[1,8,32]{2,1,0:T(8,128)S(1)} %copy.35), channel_id=1, replica_groups=mesh['batch'=4,'cache'=8] {'cache'}, dimensions={0}, use_global_device_ids=true | all-gather | bytes 9216 | tf_op jit(solution)/shard_map/all_gather | solution.py:12
  164.7 1.2 slice.49
  166.0 0.9 slice_bitcast_fusion
  166.9 1.4 while.14
  168.5 2.8 %convolution_convert_fusion.1 = bf16[8,4096]{1,0:T(8,128)(2,1)S(1)} fusion(bf16[512,4096]{1,0:T(8,128)(2,1)} %param.25, bf16[8,4096]{1,0:T(8,128)(2,1)S(1)} %bitcast.82, s32[]{:T(128)S(6)} %select_n.47), kind=kOutput, calls=%fused_computation.9 | convolution fusion | flops 33587200 | bytes 4268036 | tf_op jit(solution)/shard_map/dot_general | solution.py:131
  171.3 31.3 %all-gather = bf16[64,4096]{1,0:T(8,128)(2,1)S(1)} all-gather(bf16[8,4096]{1,0:T(8,128)(2,1)S(1)} %convolution_convert_fusion.1), channel_id=2, replica_groups=mesh['batch'=4,'cache'=8] {'cache'}, dimensions={0}, use_global_device_ids=true | all-gather | bytes 589824 | tf_op jit(solution)/shard_map/all_gather | solution.py:134
  202.8 4.2 %fusion.44 = f32[8,896]{1,0:T(8,128)S(1)} fusion(bf16[4096,896]{1,0:T(8,128)(2,1)} %param.27, bf16[8,4096]{1,0:T(8,128)(2,1)S(1)} %get-tuple-element.71, f32[4096]{0:T(1024)S(1)} %convert_element_type.107, f32[8]{0:T(128)S(1)} %add_rsqrt_fusion), kind=kOutput, calls=%fused_computation.68 | convolution fusion | flops 58851328 | bytes 7450656 | tf_op jit(solution)/shard_map/dot_general | solution.py:140
  207.0 8.1 %convolution_convert_fusion = bf16[8,4096]{1,0:T(8,128)(2,1)} fusion(bf16[896,4096]{1,0:T(8,128)(2,1)} %param.29, bf16[4096,896]{1,0:T(8,128)(2,1)} %param.28, f32[8,896]{1,0:T(8,128)S(1)} %fusion.44, bf16[8,4096]{1,0:T(8,128)(2,1)S(1)} %get-tuple-element.71, f32[4096]{0:T(1024)S(1)} %convert_element_type.107, f32[8]{0:T(128)S(1)} %add_rsqrt_fusion), kind=kOutput, calls=%fused_computation.8 | convolution fusion | flops 117647360 | bytes 14856224 | tf_op jit(solution)/shard_map/dot_general | solution.py:143
  215.1 60.3 %reduce-scatter.2.cloned.1.call-done = bf16[8,512]{1,0:T(8,128)(2,1)} async-done(((bf16[8,4096]{1,0:T(8,128)(2,1)}), bf16[8,512]{1,0:T(8,128)(2,1)}) %reduce-scatter.2.cloned.1.call-update) | async-done | bytes 8208 | tf_op jit(solution)/shard_map/reduce_scatter | solution.py:144
  275.5 1.3 add_convert_fusion.2
  (65 shorter events, 2.9 us)
Async XLA Ops:
  6.5 66.5 %copy-start = (bf16[8,128,1024]{2,1,0:T(8,128)(2,1)S(1)}, bf16[8,128,1024]{2,1,0:T(8,128)(2,1)}, u32[]{:S(2)}) copy-start(bf16[8,128,1024]{2,1,0:T(8,128)(2,1)} %param.21) | copy-start | bytes 6291460
  6.5 66.0 %copy-start.6 = (s32[8]{0:T(128)S(1)}, s32[8]{0:T(128)}, u32[]{:S(2)}) copy-start(s32[8]{0:T(128)} %param.23) | copy-start | bytes 100
  6.5 66.4 %copy-start.4 = (s32[8]{0:T(128)S(1)}, s32[8]{0:T(128)}, u32[]{:S(2)}) copy-start(s32[8]{0:T(128)} %param.24) | copy-start | bytes 100
  6.5 158.2 %all-gather.3.cloned.1.call-start = ((), (), s32[]{:S(2)}) async-start(), calls=%async_computation.1 | async-start | bytes 1179648 | tf_op jit(solution)/shard_map/all_gather | solution.py:12
  38.6 36.2 %copy-start.1 = (bf16[8,4096]{1,0:T(8,128)(2,1)S(1)}, bf16[8,4096]{1,0:T(8,128)(2,1)}, u32[]{:S(2)}) copy-start(bf16[8,4096]{1,0:T(8,128)(2,1)} %param.16) | copy-start | bytes 196612
  38.6 36.2 %copy-start.2 = (bf16[4096,128]{1,0:T(8,128)(2,1)S(1)}, bf16[4096,128]{1,0:T(8,128)(2,1)}, u32[]{:S(2)}) copy-start(bf16[4096,128]{1,0:T(8,128)(2,1)} %param.20) | copy-start | bytes 3145732
  72.4 92.2 %copy-start.3 = (bf16[4096]{0:T(1024)(128)(2,1)S(1)}, bf16[4096]{0:T(1024)(128)(2,1)}, u32[]{:S(2)}) copy-start(bf16[4096]{0:T(1024)(128)(2,1)} %param.26) | copy-start | bytes 24580
  72.6 28.7 %copy-start.5 = (bf16[8,128,1024]{2,1,0:T(8,128)(2,1)S(1)}, bf16[8,128,1024]{2,1,0:T(8,128)(2,1)}, u32[]{:S(2)}) copy-start(bf16[8,128,1024]{2,1,0:T(8,128)(2,1)} %param.22) | copy-start | bytes 6291460
  102.7 172.7 %reduce-scatter.2.cloned.1.call-start = ((), (), s32[]{:S(2)}) async-start(), calls=%async_computation.2 | async-start | bytes 73728 | tf_op jit(solution)/shard_map/reduce_scatter | solution.py:144
Sparse Core Ops, SparseCore 0:
  102.8 38.3 all-gather.2
  215.3 60.1 reduce-scatter.1
